TPU v7x, 128 devices: a whole 4x4x4 slice. The times are simulated.
128 devices in a mesh: data: 1, tp: 16 (over z, y), ep: 8 (over x, core).
Axes of the slice: x: 4, y: 4, z: 4, core: 2. Of those that a mesh axis runs over, the one named last changes fastest.
Arguments:
- tokens_a: bfloat16 [32768, 1280], P(('data', 'ep', 'tp'))
- tokens_b: bfloat16 [32768, 1280], P(('data', 'ep', 'tp'))
- experts_a: int32 [32768, 6], P(('data', 'ep', 'tp'))
- experts_b: int32 [32768, 6], P(('data', 'ep', 'tp'))
- gates_a: float32 [32768, 6], P(('data', 'ep', 'tp'))
- gates_b: float32 [32768, 6], P(('data', 'ep', 'tp'))
- slots_a: int32 [32768, 6], P(('data', 'ep', 'tp'))
- slots_b: int32 [32768, 6], P(('data', 'ep', 'tp'))
- shared_w1: bfloat16 [1280, 1792], P(None, 'tp')
- shared_w3: bfloat16 [1280, 1792], P(None, 'tp')
- shared_w2: bfloat16 [1792, 1280], P('tp')
- routed_w1: bfloat16 [64, 1280, 896], P('ep')
- routed_w3: bfloat16 [64, 1280, 896], P('ep')
- routed_w2: bfloat16 [64, 896, 1280], P('ep')
Outputs:
- output 1: bfloat16 [32768, 1280], P(('data', 'ep', 'tp'))
- output 2: bfloat16 [32768, 1280], P(('data', 'ep', 'tp'))
All inputs are finite; a program needn't handle non-finite values.
Results may differ from a plain program's by a relative error of at most 0.00503706.
Values are sent between devices in bfloat16 or wider.
A program may use at most 1 GiB of HBM per device.

v0:
```python
import jax
import jax.numpy as jnp
from jax import lax
from jax.sharding import PartitionSpec as P


def capacity_rows(tok_local, top_k, num_experts):
    return max(4, (2 * tok_local * top_k) // num_experts)


def swiglu_rows(rows, w_in, w_gate, w_out):
    proj_in = jnp.dot(rows, w_in, preferred_element_type=jnp.float32)
    proj_gate = jnp.dot(rows, w_gate, preferred_element_type=jnp.float32)
    hidden = (jax.nn.silu(proj_in) * proj_gate).astype(jnp.bfloat16)
    return jnp.dot(hidden, w_out, preferred_element_type=jnp.float32)


def solution(mesh):
    ep_size = mesh.shape['ep']
    tok_spec = P(('data', 'ep', 'tp'), None)
    in_specs = (tok_spec,) * 8 + (P(None, 'tp'), P(None, 'tp'), P('tp', None), P('ep', None, None), P('ep', None, None), P('ep', None, None))

    def shared_path(x_local, shared_w1, shared_w3, shared_w2):
        gathered = lax.all_gather(x_local, 'tp', axis=0, tiled=True)
        partial_sum = swiglu_rows(gathered, shared_w1, shared_w3, shared_w2)
        return lax.psum_scatter(partial_sum, 'tp', scatter_dimension=0, tiled=True)

    def routed_path(x_local, expert_ids, gate_vals, slot_ids, routed_w1, routed_w3, routed_w2):
        tok_local, top_k = expert_ids.shape
        local_experts, model_dim, expert_ff = routed_w1.shape
        cap_rows = capacity_rows(tok_local, top_k, local_experts * ep_size)
        num_rows = local_experts * ep_size * cap_rows
        dest_rank = expert_ids // local_experts
        local_id = expert_ids % local_experts
        keep_mask = slot_ids >= 0
        row_ids = jnp.where(keep_mask, (local_id * ep_size + dest_rank) * cap_rows + slot_ids, -1)
        place_mat = jnp.any(row_ids[:, :, None] == jnp.arange(num_rows)[None, None, :], axis=1).astype(jnp.bfloat16)
        send_rows = jnp.einsum('tr,td->rd', place_mat, x_local, preferred_element_type=jnp.float32).astype(jnp.bfloat16)
        recv_rows = lax.all_to_all(send_rows.reshape(local_experts, ep_size, cap_rows, model_dim), 'ep', 1, 1, tiled=True)
        recv_rows = recv_rows.reshape(local_experts, ep_size * cap_rows, model_dim)
        proj_in = jnp.einsum('erd,edf->erf', recv_rows, routed_w1, preferred_element_type=jnp.float32)
        proj_gate = jnp.einsum('erd,edf->erf', recv_rows, routed_w3, preferred_element_type=jnp.float32)
        hidden = (jax.nn.silu(proj_in) * proj_gate).astype(jnp.bfloat16)
        expert_out = jnp.einsum('erf,efd->erd', hidden, routed_w2, preferred_element_type=jnp.float32).astype(jnp.bfloat16)
        back_rows = lax.all_to_all(expert_out.reshape(local_experts, ep_size, cap_rows, model_dim), 'ep', 1, 1, tiled=True)
        picked = jnp.take(back_rows.reshape(num_rows, model_dim), jnp.maximum(row_ids, 0), axis=0)
        weights = jnp.where(keep_mask, gate_vals, 0.0)
        return jnp.sum(picked.astype(jnp.float32) * weights[:, :, None], axis=1)

    def layer_local(tokens_a, tokens_b, experts_a, experts_b, gates_a, gates_b, slots_a, slots_b, shared_w1, shared_w3, shared_w2, routed_w1, routed_w3, routed_w2):
        def one_microbatch(x_local, expert_ids, gate_vals, slot_ids):
            shared_out = shared_path(x_local, shared_w1, shared_w3, shared_w2)
            routed_out = routed_path(x_local, expert_ids, gate_vals, slot_ids, routed_w1, routed_w3, routed_w2)
            return (x_local.astype(jnp.float32) + shared_out + routed_out).astype(jnp.bfloat16)
        out_a = one_microbatch(tokens_a, experts_a, gates_a, slots_a)
        out_b = one_microbatch(tokens_b, experts_b, gates_b, slots_b)
        return (out_a, out_b)

    return jax.shard_map(layer_local, mesh=mesh, in_specs=in_specs, out_specs=(tok_spec, tok_spec), check_vma=False)
```

profile of v0, /device:TPU:1, one launch (start us, length us, event | category | flops | bytes accessed | tf_op | source)
XLA Modules:
  0.0 648.4 jit_solution(2061601845851909895)
XLA Ops:
  7.2 0.0 copy-start
  7.2 0.0 all-gather.5.cloned.1.call-start
  7.2 0.7 all-gather.5.cloned.1.call-update
  7.9 0.0 all-gather.3.cloned.1.call-start
  8.0 0.7 all-gather.3.cloned.1.call-update
  8.7 0.0 reduce-scatter.5.cloned.1.call-start
  8.7 84.8 %all-gather.5.cloned.1.call-done = bf16[4096,1280]{1,0:T(8,128)(2,1)} async-done(((bf16[256,1280]{1,0:T(8,128)(2,1)}), bf16[4096,1280]{1,0:T(8,128)(2,1)}) %all-gather.5.cloned.1.call-update) | async-done | bytes 10485776 | tf_op jit(solution)/shard_map/all_gather | solution.py:24
  93.5 7.3 %fusion.46 = f32[4096,112]{0,1:T(8,128)S(1)} fusion(bf16[4096,1280]{1,0:T(8,128)(2,1)} %all-gather.5.cloned.1.call-done, bf16[1280,112]{0,1:T(8,128)(2,1)} %param.24), kind=kOutput, calls=%fused_computation.80 | convolution fusion | flops 1174405120 | bytes 12607488 | tf_op jit(solution)/shard_map/dot_general | solution.py:12
  100.9 17.2 %fusion.10 = f32[4096,1280]{1,0:T(8,128)} fusion(bf16[112,1280]{1,0:T(8,128)(2,1)S(1)} %copy-done, bf16[4096,1280]{1,0:T(8,128)(2,1)} %all-gather.5.cloned.1.call-done, bf16[1280,112]{0,1:T(8,128)(2,1)S(1)} %copy-done.9, f32[4096,112]{0,1:T(8,128)S(1)} %fusion.46), kind=kOutput, calls=%fused_computation.22 | convolution fusion | flops 2351562752 | bytes 33865728 | tf_op jit(solution)/shard_map/dot_general | solution.py:15
  118.1 0.0 reduce-scatter.5.cloned.1.call-update
  118.1 0.6 reduce-scatter.3.cloned.1.call-start
  118.7 57.1 %all-gather.3.cloned.1.call-done = bf16[4096,1280]{1,0:T(8,128)(2,1)} async-done(((bf16[256,1280]{1,0:T(8,128)(2,1)}), bf16[4096,1280]{1,0:T(8,128)(2,1)}) %all-gather.3.cloned.1.call-update) | async-done | bytes 10485776 | tf_op jit(solution)/shard_map/all_gather | solution.py:24
  175.7 7.3 %fusion.44 = f32[4096,112]{0,1:T(8,128)S(1)} fusion(bf16[4096,1280]{1,0:T(8,128)(2,1)} %all-gather.3.cloned.1.call-done, bf16[1280,112]{0,1:T(8,128)(2,1)S(1)} %copy-done.10), kind=kOutput, calls=%fused_computation.78 | convolution fusion | flops 1174405120 | bytes 12607488 | tf_op jit(solution)/shard_map/dot_general | solution.py:12
  183.0 17.2 %fusion.14 = f32[4096,1280]{1,0:T(8,128)} fusion(bf16[112,1280]{1,0:T(8,128)(2,1)S(1)} %copy-done, bf16[4096,1280]{1,0:T(8,128)(2,1)} %all-gather.3.cloned.1.call-done, bf16[1280,112]{0,1:T(8,128)(2,1)S(1)} %copy-done.9, f32[4096,112]{0,1:T(8,128)S(1)} %fusion.44), kind=kOutput, calls=%fused_computation.26 | convolution fusion | flops 2351562752 | bytes 33865728 | tf_op jit(solution)/shard_map/dot_general | solution.py:15
  200.2 0.0 reduce-scatter.3.cloned.1.call-update
  200.3 0.7 copy-done.11
  200.9 0.0 copy-done.15
  201.0 4.2 fusion.1
  205.2 3.1 convolution_convert_fusion
  208.3 3.7 copy.54
  212.0 5.8 all-to-all-start.2
  217.7 0.0 copy-done.12
  217.8 4.2 fusion
  222.0 0.0 copy-done.7
  222.0 2.9 convolution_convert_fusion.1
  224.9 3.8 copy.47
  228.7 77.0 %all-to-all-done.2 = bf16[8,8,48,1280]{3,2,0,1:T(8,128)(2,1)} async-done(((bf16[8,8,48,1280]{3,2,0,1:T(8,128)(2,1)}), bf16[8,8,48,1280]{3,2,0,1:T(8,128)(2,1)}, u32[]{:S(2)}, u32[]{:S(2)}) %all-to-all-start.2) | async-done | bytes 7864352 | tf_op jit(solution)/shard_map/all_to_all | solution.py:39
  305.7 6.1 all-to-all-start
  311.8 3.9 copy.55
  315.7 3.1 copy-done.3
  318.8 14.5 %fusion.47 = f32[8,384,896]{2,1,0:T(8,128)} fusion(bf16[8,384,1280]{2,1,0:T(8,128)(2,1)S(1)} %bitcast.36, bf16[8,1280,896]{2,1,0:T(8,128)(2,1)} %param.27), kind=kOutput, calls=%fused_computation.81 | convolution fusion | flops 7046430720 | bytes 37224448 | tf_op jit(solution)/shard_map/erd,edf->erf/dot_general | solution.py:41
  333.3 25.5 %convolution_convert_fusion.2 = bf16[8,384,1280]{2,1,0:T(8,128)(2,1)} fusion(bf16[8,896,1280]{2,1,0:T(8,128)(2,1)} %param.29, f32[8,384,896]{2,1,0:T(8,128)} %fusion.47, bf16[8,384,1280]{2,1,0:T(8,128)(2,1)} %bitcast.37, bf16[8,1280,896]{2,1,0:T(8,128)(2,1)} %param.28), kind=kOutput, calls=%fused_computation.12 | convolution fusion | flops 14113308672 | bytes 63438848 | tf_op jit(solution)/shard_map/erf,efd->erd/dot_general | solution.py:44
  358.8 7.1 %copy.56 = bf16[8,8,48,1280]{3,2,0,1:T(8,128)(2,1)} copy(bf16[8,8,48,1280]{3,2,1,0:T(8,128)(2,1)} %bitcast.38) | data formatting | bytes 15728640 | tf_op jit(solution)/shard_map/reshape | solution.py:45
  365.9 33.8 %all-to-all-done = bf16[8,8,48,1280]{3,2,0,1:T(8,128)(2,1)} async-done(((bf16[8,8,48,1280]{3,2,0,1:T(8,128)(2,1)}), bf16[8,8,48,1280]{3,2,0,1:T(8,128)(2,1)}, u32[]{:S(2)}, u32[]{:S(2)}) %all-to-all-start) | async-done | bytes 7864352 | tf_op jit(solution)/shard_map/all_to_all | solution.py:39
  399.7 6.2 all-to-all-start.3
  405.8 3.9 copy.48
  409.7 3.2 copy-done.4
  412.9 14.5 %fusion.45 = f32[8,384,896]{2,1,0:T(8,128)} fusion(bf16[8,384,1280]{2,1,0:T(8,128)(2,1)S(1)} %bitcast.39, bf16[8,1280,896]{2,1,0:T(8,128)(2,1)} %param.27), kind=kOutput, calls=%fused_computation.79 | convolution fusion | flops 7046430720 | bytes 37224448 | tf_op jit(solution)/shard_map/erd,edf->erf/dot_general | solution.py:41
  427.4 25.6 %convolution_convert_fusion.3 = bf16[8,384,1280]{2,1,0:T(8,128)(2,1)} fusion(bf16[8,896,1280]{2,1,0:T(8,128)(2,1)} %param.29, f32[8,384,896]{2,1,0:T(8,128)} %fusion.45, bf16[8,384,1280]{2,1,0:T(8,128)(2,1)} %bitcast.40, bf16[8,1280,896]{2,1,0:T(8,128)(2,1)} %param.28), kind=kOutput, calls=%fused_computation.13 | convolution fusion | flops 14113308672 | bytes 63438848 | tf_op jit(solution)/shard_map/erf,efd->erd/dot_general | solution.py:44
  453.0 7.0 %copy.49 = bf16[8,8,48,1280]{3,2,0,1:T(8,128)(2,1)} copy(bf16[8,8,48,1280]{3,2,1,0:T(8,128)(2,1)} %bitcast.41) | data formatting | bytes 15728640 | tf_op jit(solution)/shard_map/reshape | solution.py:45
  460.0 33.7 %all-to-all-done.3 = bf16[8,8,48,1280]{3,2,0,1:T(8,128)(2,1)} async-done(((bf16[8,8,48,1280]{3,2,0,1:T(8,128)(2,1)}), bf16[8,8,48,1280]{3,2,0,1:T(8,128)(2,1)}, u32[]{:S(2)}, u32[]{:S(2)}) %all-to-all-start.3) | async-done | bytes 7864352 | tf_op jit(solution)/shard_map/all_to_all | solution.py:45
  493.7 6.2 all-to-all-start.1
  499.9 0.1 copy.58
  500.0 0.1 reshape.69
  500.2 0.2 copy.53
  500.4 0.0 copy-done.13
  500.4 0.1 copy.59
  500.5 0.1 copy.51
  500.7 0.1 reshape.65
  500.8 0.2 copy.46
  501.0 0.0 copy-done.14
  501.0 0.1 copy.52
  501.2 7.2 %copy.57 = bf16[8,8,48,1280]{3,2,1,0:T(8,128)(2,1)} copy(bf16[8,8,48,1280]{3,2,0,1:T(8,128)(2,1)} %all-to-all-done.3) | data formatting | bytes 15728640 | tf_op jit(solution)/shard_map/all_to_all | solution.py:45
  508.4 13.3 %gather_fusion.1 = bf16[1536,1280]{1,0:T(8,128)(2,1)} fusion(bf16[3072,1280]{1,0:T(8,128)(2,1)} %bitcast.32, s32[2048]{0:T(1024)S(1)} %pad_clamp_fusion), kind=kCustom, calls=%fused_computation.1.clone | custom fusion | bytes 7870464 | tf_op jit(solution)/shard_map/jit(_take)/gather | solution.py:46
  521.7 7.1 %reshape.72 = bf16[256,6,1280]{2,1,0:T(8,128)(2,1)} reshape(bf16[1536,1280]{1,0:T(8,128)(2,1)} %gather_fusion.1) | data formatting | bytes 7864320 | tf_op jit(solution)/shard_map/jit(_take)/gather | solution.py:46
  528.7 59.0 %all-to-all-done.1 = bf16[8,8,48,1280]{3,2,0,1:T(8,128)(2,1)} async-done(((bf16[8,8,48,1280]{3,2,0,1:T(8,128)(2,1)}), bf16[8,8,48,1280]{3,2,0,1:T(8,128)(2,1)}, u32[]{:S(2)}, u32[]{:S(2)}) %all-to-all-start.1) | async-done | bytes 7864352 | tf_op jit(solution)/shard_map/all_to_all | solution.py:45
  587.8 7.0 %copy.50 = bf16[8,8,48,1280]{3,2,1,0:T(8,128)(2,1)} copy(bf16[8,8,48,1280]{3,2,0,1:T(8,128)(2,1)} %all-to-all-done.1) | data formatting | bytes 15728640 | tf_op jit(solution)/shard_map/all_to_all | solution.py:45
  594.8 13.3 %gather_fusion = bf16[1536,1280]{1,0:T(8,128)(2,1)} fusion(bf16[3072,1280]{1,0:T(8,128)(2,1)} %bitcast.33, s32[2048]{0:T(1024)S(1)} %pad_clamp_fusion.1), kind=kCustom, calls=%fused_computation.clone | custom fusion | bytes 7870464 | tf_op jit(solution)/shard_map/jit(_take)/gather | solution.py:46
  608.0 7.1 %reshape.68 = bf16[256,6,1280]{2,1,0:T(8,128)(2,1)} reshape(bf16[1536,1280]{1,0:T(8,128)(2,1)} %gather_fusion) | data formatting | bytes 7864320 | tf_op jit(solution)/shard_map/jit(_take)/gather | solution.py:46
  615.2 7.9 %multiply_reduce_fusion = f32[256,1280]{1,0:T(8,128)} fusion(bf16[256,6,1280]{2,1,0:T(8,128)(2,1)} %reshape.72, f32[256,6]{1,0:T(8,128)S(1)} %copy.59, pred[256,6]{1,0:T(8,128)(4,1)S(1)} %copy.53), kind=kLoop, calls=%fused_computation.10 | loop fusion | flops 7536640 | bytes 5250560 | tf_op jit(solution)/shard_map/reduce_sum | solution.py:48
  623.0 13.0 %multiply_reduce_fusion.1 = f32[256,1280]{1,0:T(8,128)S(1)} fusion(bf16[256,6,1280]{2,1,0:T(8,128)(2,1)S(1)} %copy-done.2, f32[256,6]{1,0:T(8,128)S(1)} %copy.52, pred[256,6]{1,0:T(8,128)(4,1)S(1)} %copy.46), kind=kLoop, calls=%fused_computation.11 | loop fusion | flops 7536640 | bytes 5250560 | tf_op jit(solution)/shard_map/reduce_sum | solution.py:48
  636.0 0.0 reduce-scatter.5.cloned.1.call-done
  636.1 2.8 add_convert_fusion
  638.8 2.4 add_convert_fusion.1
  (34 shorter events, 0.1 us)
Async XLA Ops:
  7.2 93.7 %copy-start = (bf16[112,1280]{1,0:T(8,128)(2,1)S(1)}, bf16[112,1280]{1,0:T(8,128)(2,1)}, u32[]{:S(2)}) copy-start(bf16[112,1280]{1,0:T(8,128)(2,1)} %param.26) | copy-start | bytes 860164
  7.2 86.4 %all-gather.5.cloned.1.call-start = ((), (), s32[]{:S(2)}) async-start(), calls=%async_computation.8 | async-start | bytes 11141120 | tf_op jit(solution)/shard_map/all_gather | solution.py:24
  7.9 92.9 %copy-start.9 = (bf16[1280,112]{0,1:T(8,128)(2,1)S(1)}, bf16[1280,112]{0,1:T(8,128)(2,1)}, u32[]{:S(2)}) copy-start(bf16[1280,112]{0,1:T(8,128)(2,1)} %param.25) | copy-start | bytes 860164
  7.9 167.8 %all-gather.3.cloned.1.call-start = ((), (), s32[]{:S(2)}) async-start(), calls=%async_computation.6 | async-start | bytes 11141120 | tf_op jit(solution)/shard_map/all_gather | solution.py:24
  8.7 627.4 %reduce-scatter.5.cloned.1.call-start = ((), (), s32[]{:S(2)}) async-start(), calls=%async_computation.9 | async-start | bytes 22282240 | tf_op jit(solution)/shard_map/reduce_scatter | solution.py:26
  118.1 57.7 %copy-start.10 = (bf16[1280,112]{0,1:T(8,128)(2,1)S(1)}, bf16[1280,112]{0,1:T(8,128)(2,1)}, u32[]{:S(2)}) copy-start(bf16[1280,112]{0,1:T(8,128)(2,1)} %param.24) | copy-start | bytes 860164
  118.1 520.8 %reduce-scatter.3.cloned.1.call-start = ((), (), s32[]{:S(2)}) async-start(), calls=%async_computation.7 | async-start | bytes 22282240 | tf_op jit(solution)/shard_map/reduce_scatter | solution.py:26
  200.2 0.7 copy-start.11
  200.2 0.7 copy-start.15
  200.2 5.0 copy-start.5
  212.0 5.8 copy-start.12
  212.0 5.8 copy-start.16
  212.0 10.1 %copy-start.7 = (bf16[256,1280]{1,0:T(8,128)(2,1)S(1)}, bf16[256,1280]{1,0:T(8,128)(2,1)}, u32[]{:S(2)}) copy-start(bf16[256,1280]{1,0:T(8,128)(2,1)} %param.16) | copy-start | bytes 1966084
  212.0 93.7 %all-to-all-start.2 = ((bf16[8,8,48,1280]{3,2,0,1:T(8,128)(2,1)}), bf16[8,8,48,1280]{3,2,0,1:T(8,128)(2,1)}, u32[]{:S(2)}, u32[]{:S(2)}) async-start(bf16[8,8,48,1280]{3,2,0,1:T(8,128)(2,1)} %copy.54), calls=%async_computation.4 | async-start | bytes 15728640 | tf_op jit(solution)/shard_map/all_to_all | solution.py:39
  305.7 94.0 %all-to-all-start = ((bf16[8,8,48,1280]{3,2,0,1:T(8,128)(2,1)}), bf16[8,8,48,1280]{3,2,0,1:T(8,128)(2,1)}, u32[]{:S(2)}, u32[]{:S(2)}) async-start(bf16[8,8,48,1280]{3,2,0,1:T(8,128)(2,1)} %copy.47), calls=%async_computation.1 | async-start | bytes 15728640 | tf_op jit(solution)/shard_map/all_to_all | solution.py:39
  315.7 3.1 copy-start.3
  399.7 94.1 %all-to-all-start.3 = ((bf16[8,8,48,1280]{3,2,0,1:T(8,128)(2,1)}), bf16[8,8,48,1280]{3,2,0,1:T(8,128)(2,1)}, u32[]{:S(2)}, u32[]{:S(2)}) async-start(bf16[8,8,48,1280]{3,2,0,1:T(8,128)(2,1)} %copy.56), calls=%async_computation.5 | async-start | bytes 15728640 | tf_op jit(solution)/shard_map/all_to_all | solution.py:45
  409.7 3.2 copy-start.4
  460.0 40.3 %copy-start.13 = (f32[256,6]{0,1:T(8,128)S(1)}, f32[256,6]{0,1:T(8,128)}, u32[]{:S(2)}) copy-start(f32[256,6]{0,1:T(8,128)} %param.21) | copy-start | bytes 18436
  460.0 41.0 %copy-start.14 = (f32[256,6]{0,1:T(8,128)S(1)}, f32[256,6]{0,1:T(8,128)}, u32[]{:S(2)}) copy-start(f32[256,6]{0,1:T(8,128)} %param.20) | copy-start | bytes 18436
  493.7 94.0 %all-to-all-start.1 = ((bf16[8,8,48,1280]{3,2,0,1:T(8,128)(2,1)}), bf16[8,8,48,1280]{3,2,0,1:T(8,128)(2,1)}, u32[]{:S(2)}, u32[]{:S(2)}) async-start(bf16[8,8,48,1280]{3,2,0,1:T(8,128)(2,1)} %copy.49), calls=%async_computation.2 | async-start | bytes 15728640 | tf_op jit(solution)/shard_map/all_to_all | solution.py:45
  615.2 7.9 %copy-start.2 = (bf16[256,6,1280]{2,1,0:T(8,128)(2,1)S(1)}, bf16[256,6,1280]{2,1,0:T(8,128)(2,1)}, u32[]{:S(2)}) copy-start(bf16[256,6,1280]{2,1,0:T(8,128)(2,1)} %reshape.68) | copy-start | bytes 11796484
  615.2 20.9 %copy-start.6 = (bf16[256,1280]{1,0:T(8,128)(2,1)S(1)}, bf16[256,1280]{1,0:T(8,128)(2,1)}, u32[]{:S(2)}) copy-start(bf16[256,1280]{1,0:T(8,128)(2,1)} %param.17) | copy-start | bytes 1966084
  615.2 23.7 %copy-start.8 = (bf16[256,1280]{1,0:T(8,128)(2,1)S(1)}, bf16[256,1280]{1,0:T(8,128)(2,1)}, u32[]{:S(2)}) copy-start(bf16[256,1280]{1,0:T(8,128)(2,1)} %param.16) | copy-start | bytes 1966084
  615.2 26.1 %copy-start.1 = (bf16[112,1280]{1,0:T(8,128)(2,1)S(1)}, bf16[112,1280]{1,0:T(8,128)(2,1)}, u32[]{:S(2)}) copy-start(bf16[112,1280]{1,0:T(8,128)(2,1)} %param.26) | copy-start | bytes 860164
Sparse Core Ops, SparseCore 0:
  10.1 83.3 all-gather.4
  95.7 79.9 all-gather.2
  179.2 131.4 reduce-scatter.4
  314.0 131.4 reduce-scatter.2
where the time goes:
time: 654 us; the launch traced here: 648 us
  waiting for transfers between devices  347 us (53%)
  matrix products  135 us (21%)
  local copies, waits for them, and re-layouts  92.5 us (14%)
  other arithmetic  34.5 us (5%)
  starting transfers between devices  24.9 us (4%)
  between operations  14.7 us (2%)
    all_gather x2, waiting for transfers between devices, shared_path(): gathered = lax.all_gather(x_local, 'tp', axis=0, tiled=True)  142 us
    all_to_all x2, waiting for transfers between devices, routed_path(): lax.all_to_all(send_rows.reshape(local_experts, ep_size, cap_rows, model_...  111 us
    all_to_all x2, waiting for transfers between devices, routed_path(): lax.all_to_all(expert_out.reshape(local_experts, ep_size, cap_rows, model...  92.7 us
    dot_general x2, matrix products, routed_path(): jnp.einsum('erf,efd->erd', hidden, routed_w2, preferred_element_type=jnp....  51.2 us
    gather x4, local copies, waits for them, and re-layouts, routed_path(): jnp.take(back_rows.reshape(num_rows, model_dim), jnp.maximum(row_ids, 0),...  40.8 us
    dot_general x2, matrix products, swiglu_rows(): return jnp.dot(hidden, w_out, preferred_element_type=jnp.float32)  34.4 us
    dot_general x2, matrix products, routed_path(): jnp.einsum('erd,edf->erf', recv_rows, routed_w1, preferred_element_type=j...  29 us
    reduce_sum x2, other arithmetic, routed_path(): return jnp.sum(picked.astype(jnp.float32) * weights[:, :, None], axis=1)  20.8 us
  transfers between devices with their start and end apart: 8, of which 6 were waited for; matrix products, arithmetic and copies ran while one was open for 39% of the time, Pallas kernels for 0%

commit v1 on v0

v1 whole, which is shorter than its diff:
```python
import functools

import jax
import jax.numpy as jnp
from jax import lax
from jax.experimental import pallas as pl
from jax.experimental.pallas import tpu as pltpu
from jax.sharding import PartitionSpec as P

MESH = pl.DeviceIdType.MESH
F32 = jnp.float32
BF16 = jnp.bfloat16


def _split_gate(gate):
    high = gate.astype(BF16)
    rest = gate - high.astype(F32)
    middle = rest.astype(BF16)
    low = (rest - middle.astype(F32)).astype(BF16)
    return high, middle, low


def _layer_kernel(
    cap, top_k,
    tok_a, tok_b, meta_in, shared_in, routed_w1, routed_w3, routed_w2,
    out_a, out_b, far_hbm, gath_hbm,
    near, stage, meta, rows, w13, w2, hid, pair_out, pair_in, sums, turn_p, turn_m, last_p, last_m,
    sem_near, sem_near_recv, sem_meta_send, sem_meta_recv, sem_ag_send, sem_ag_recv, sem_stage, sem_w,
    sem_sh_send, sem_sh_recv, sem_sh_own, sem_sh_load, sem_pair_send, sem_pair_recv, sem_rs_send, sem_rs_recv, pair_free,
):
    local_experts, model_dim, ff = routed_w1.shape
    tok = tok_a.shape[0]
    half = tok // 2
    shard = shared_in.shape[1]
    num_rows = local_experts * cap
    tile = 256
    n_tiles = model_dim // tile
    f_tiles = ff // 128

    ep = lax.axis_index('ep')
    tp = lax.axis_index('tp')
    chip, core = ep // 2, lax.rem(ep, 2)
    z, y = tp // 4, lax.rem(tp, 4)

    def on_x(step, other=0):
        side = core if other == 0 else 1 - core
        return {'ep': lax.rem(chip + step, 4) * 2 + side, 'tp': tp}

    def on_y(step):
        return {'ep': ep, 'tp': z * 4 + lax.rem(y + step, 4)}

    def on_z(step):
        return {'ep': ep, 'tp': lax.rem(z + step, 4) * 4 + y}

    def remote(src, dst, send, recv, device):
        return pltpu.make_async_remote_copy(src_ref=src, dst_ref=dst, send_sem=send, recv_sem=recv, device_id=device, device_id_type=MESH)

    low, high = pl.ds(0, half), pl.ds(half, half)

    tokens = (tok_a, tok_b)

    def ag_own(m, k):
        part, step, slot = ((low, 1, 6), (high, 1, 6), (high, 3, 2), (low, 3, 2))[k]
        return remote(tokens[m].at[part], far_hbm.at[m, slot, part], sem_ag_send.at[m, k], sem_ag_recv.at[m, k], on_x(step))

    def ag_relay(m, k):
        part, step, slot = ((low, 1, 6), (high, 3, 2))[k]
        return remote(far_hbm.at[m, slot, part], far_hbm.at[m, 4, part], sem_ag_send.at[m, 4 + k], sem_ag_recv.at[m, 4 + k], on_x(step))

    def ag_pair(m, k):
        slot = (6, 2, 4)[k]
        return remote(far_hbm.at[m, slot], far_hbm.at[m, slot + 1], sem_ag_send.at[m, 6 + k], sem_ag_recv.at[m, 6 + k], on_x(0, 1))

    def near_pair(m):
        return remote(tokens[m], near.at[2 * m + 1], sem_near.at[m], sem_near_recv.at[m], on_x(0, 1))

    def near_own(m):
        return pltpu.make_async_copy(tokens[m], near.at[2 * m], sem_near.at[2 + m])

    def meta_send(dx, other):
        back = (4 - dx) % 4
        slot = back * 2 + other
        return remote(meta_in, meta.at[slot], sem_meta_send.at[dx * 2 + other], sem_meta_recv.at[slot], on_x(dx, other))

    meta_own = pltpu.make_async_copy(meta_in, meta.at[0], sem_meta_send.at[0])
    others = [(dx, other) for dx in range(4) for other in range(2) if (dx, other) != (0, 0)]

    mine = lax.rem(y, 2) == core
    own_slot = z * 2 + y // 2

    def shard_y(k):
        return remote(shared_in, gath_hbm.at[own_slot], sem_sh_send.at[k], sem_sh_recv.at[own_slot], on_y((1, 3, 2)[k]))

    shard_own = pltpu.make_async_copy(shared_in, gath_hbm.at[own_slot], sem_sh_own)

    def shard_wait(slot):
        pltpu.make_async_copy(shared_in, gath_hbm.at[slot], sem_sh_recv.at[slot]).wait()

    def shard_z(k):
        slot = z * 2 + k % 2
        return remote(gath_hbm.at[slot], gath_hbm.at[slot], sem_sh_send.at[3 + k], sem_sh_recv.at[slot], on_z((1, 3)[k // 2]))

    def shard_relay(k):
        slot = lax.rem(z + (3, 1)[k], 4) * 2 + k
        return remote(gath_hbm.at[slot], gath_hbm.at[slot], sem_sh_send.at[7 + k], sem_sh_recv.at[slot], on_z((1, 3)[k]))

    def weights(buf, expert, act):
        for j in range(f_tiles):
            col = pl.ds(128 * j, 128)
            act(pltpu.make_async_copy(routed_w1.at[expert, :, col], w13.at[buf, j, :, pl.ds(0, 128)], sem_w.at[buf, 2 * j]))
            act(pltpu.make_async_copy(routed_w3.at[expert, :, col], w13.at[buf, j, :, pl.ds(128, 128)], sem_w.at[buf, 2 * j + 1]))
        act(pltpu.make_async_copy(routed_w2.at[expert], w2.at[buf], sem_w.at[buf, 2 * f_tiles]))

    def pair_copy(n):
        k = lax.rem(n, 2)
        return remote(pair_out.at[k], pair_in.at[k], sem_pair_send.at[n], sem_pair_recv.at[n], on_x(0, 1))

    def rs_turn(m, k):
        part, step, dst = ((low, 1, turn_p), (high, 3, turn_m))[k]
        return remote(sums.at[m, 0, part], dst.at[m], sem_rs_send.at[m, k], sem_rs_recv.at[m, k], on_x(step))

    def rs_last(m, k):
        part, step, dst, i = ((high, 1, last_m, 1), (low, 3, last_p, 2), (low, 1, last_m, 1), (high, 3, last_p, 2))[k]
        return remote(sums.at[m, i, part], dst.at[m, part], sem_rs_send.at[m, 2 + k], sem_rs_recv.at[m, 2 + k], on_x(step))

    def hits_of(slot, m):
        ids = meta[slot, 2 * m] - (ep * num_rows).astype(F32)
        row = lax.broadcasted_iota(jnp.int32, (num_rows, tok), 0).astype(F32)
        return [row == ids[j:j + 1, :] for j in range(top_k)]

    def place(q, slot, m, src, src_index):
        hits = hits_of(slot, m)
        matrix = functools.reduce(jnp.logical_or, hits)
        matrix = jnp.where(matrix, 1.0, 0.0).astype(BF16)
        for n in range(n_tiles):
            col = pl.ds(n * tile, tile)
            picked = jnp.dot(matrix, src[src_index, :, col], preferred_element_type=F32).astype(BF16)
            rows[:, q, :, col] = picked.reshape(local_experts, cap, tile)

    def ffn(expert, count, q0, nq):
        buf = lax.rem(count, 2)
        weights(buf, expert, lambda c: c.wait())

        @pl.when(count + 1 < 3 * local_experts)
        def _():
            weights(1 - buf, lax.rem(expert + 1, local_experts), lambda c: c.start())

        size = nq * cap
        x = rows[expert, pl.ds(q0, nq)].reshape(size, model_dim)
        for j in range(f_tiles):
            both = jnp.dot(x, w13[buf, j], preferred_element_type=F32)
            hid[pl.ds(0, size), pl.ds(128 * j, 128)] = (jax.nn.silu(both[:, :128]) * both[:, 128:]).astype(BF16)
        h = hid[pl.ds(0, size), :]
        for n in range(n_tiles):
            col = pl.ds(n * tile, tile)
            res = jnp.dot(h, w2[buf, :, col], preferred_element_type=F32).astype(BF16)
            rows[expert, pl.ds(q0, nq), :, col] = res.reshape(nq, cap, tile)

    def combine(q, slot, m, dst, add):
        gates = meta[slot, 2 * m + 1]
        matrix = 0.0
        for j, hit in enumerate(hits_of(slot, m)):
            matrix = matrix + jnp.where(hit, gates[j:j + 1, :], 0.0)
        matrix = jnp.concatenate(_split_gate(matrix), axis=0)
        for n in range(n_tiles):
            col = pl.ds(n * tile, tile)
            res = rows[:, q, :, col].reshape(num_rows, tile)
            res = jnp.concatenate([res, res, res], axis=0)
            part = lax.dot_general(matrix, res, (((0,), (0,)), ((), ())), preferred_element_type=F32)
            dst[:, col] = dst[:, col] + part if add else part

    def add_into(dst, src):
        step = min(32, dst.shape[0])

        def body(i, carry):
            part = pl.ds(pl.multiple_of(i * step, step), step)
            dst[part, :] = dst[part, :] + src[part, :]
            return carry
        lax.fori_loop(0, dst.shape[0] // step, body, 0)

    def shared(q, dst):
        x = near[q]
        width = min(tile, ff)
        dims = (((1,), (1,)), ((), ()))
        for start in range(0, ff, width):
            size = min(width, ff - start)
            row = pl.ds(start, size)
            a = lax.dot_general(x, w2[0, row, :], dims, preferred_element_type=F32)
            g = lax.dot_general(x, w2[1, row, :], dims, preferred_element_type=F32)
            hid[pl.ds(0, tok), row] = (jax.nn.silu(a) * g).astype(BF16)
        h = hid[pl.ds(0, tok), :]
        for n in range(n_tiles):
            dst[:, pl.ds(n * tile, tile)] = jnp.dot(h, w13[0, n, pl.ds(0, ff), :], preferred_element_type=F32)

    def shared_load(act):
        def body(k, carry):
            row = pl.ds(pl.multiple_of(k * shard, shard), shard)
            act(pltpu.make_async_copy(gath_hbm.at[k, 0], w2.at[0, row], sem_sh_load.at[k, 0]))
            act(pltpu.make_async_copy(gath_hbm.at[k, 1], w2.at[1, row], sem_sh_load.at[k, 1]))
            for n in range(n_tiles):
                act(pltpu.make_async_copy(gath_hbm.at[k, 2, :, pl.ds(n * tile, tile)], w13.at[0, n, row], sem_sh_load.at[k, 2 + n]))
            return carry
        lax.fori_loop(0, 8, body, 0)

    weights(0, 0, lambda c: c.start())
    near_own(0).start()
    near_own(1).start()
    meta_own.start()
    barrier = pltpu.get_barrier_semaphore()
    peers = [on_x(dx, other) for dx, other in others] + [on_y(1), on_y(2), on_y(3), on_z(1), on_z(3)]
    for peer in peers:
        pl.semaphore_signal(barrier, inc=1, device_id=peer, device_id_type=MESH)
    pl.semaphore_wait(barrier, len(peers))

    for k in (0, 2, 1, 3):
        ag_own(0, k).start()
    near_pair(0).start()
    near_pair(1).start()
    for dx, other in others:
        meta_send(dx, other).start()

    @pl.when(mine)
    def _():
        for k in range(3):
            shard_y(k).start()
        shard_own.start()

    meta_own.wait()
    near_own(0).wait()
    near_own(1).wait()
    near_pair(0).wait_recv()
    near_pair(1).wait_recv()
    meta_send(0, 1).wait_recv()

    def place_near(q, carry):
        place(q, lax.rem(q, 2), q // 2, near, q)
        return carry
    lax.fori_loop(0, 4, place_near, 0)

    def ffn_near(e, carry):
        @pl.when(e == 2)
        def _():
            ag_own(0, 0).wait_recv()
            ag_relay(0, 0).start()
            ag_own(0, 2).wait_recv()
            ag_relay(0, 1).start()
            for k in (0, 2, 1, 3):
                ag_own(1, k).start()

        @pl.when(e == 5)
        def _():
            ag_own(0, 1).wait_recv()
            ag_pair(0, 0).start()
            ag_own(0, 3).wait_recv()
            ag_pair(0, 1).start()

        @pl.when(e == 7)
        def _():
            for h in range(2):
                owned = jnp.logical_and(mine, y // 2 == h)

                @pl.when(owned)
                def _():
                    shard_own.wait()

                @pl.when(jnp.logical_not(owned))
                def _():
                    shard_wait(z * 2 + h)
            for k in range(4):
                shard_z(k).start()
        ffn(e, e, 0, 4)
        return carry
    lax.fori_loop(0, local_experts, ffn_near, 0)

    for dx, other in others[1:]:
        meta_send(dx, other).wait_recv()
    ag_relay(0, 0).wait_recv()
    ag_relay(0, 1).wait_recv()
    ag_pair(0, 2).start()

    def turn(m):
        rs_turn(m, 0).wait_recv()
        add_into(sums.at[m, 1, low], turn_p.at[m])
        rs_last(m, 2).start()
        rs_turn(m, 1).wait_recv()
        add_into(sums.at[m, 2, high], turn_m.at[m])
        rs_last(m, 3).start()

    def stage_copy(m, i):
        k = lax.rem(i, 2)
        return pltpu.make_async_copy(far_hbm.at[m, i + 2], stage.at[k], sem_stage.at[k])

    def far(m, carry):
        for k in range(3):
            ag_pair(m, k).wait_recv()
        stage_copy(m, 0).start()

        def place_far(i, carry):
            stage_copy(m, i).wait()

            @pl.when(i < 5)
            def _():
                stage_copy(m, i + 1).start()
            place(4 + 6 * m + i, 2 + i, m, stage, lax.rem(i, 2))
            return carry
        lax.fori_loop(0, 6, place_far, 0)

        def ffn_far(e, carry):
            @pl.when(jnp.logical_and(m == 0, e == 1))
            def _():
                ag_own(1, 0).wait_recv()
                ag_relay(1, 0).start()
                ag_own(1, 2).wait_recv()
                ag_relay(1, 1).start()

            @pl.when(jnp.logical_and(m == 0, e == 4))
            def _():
                ag_own(1, 1).wait_recv()
                ag_pair(1, 0).start()
                ag_own(1, 3).wait_recv()
                ag_pair(1, 1).start()

            @pl.when(jnp.logical_and(m == 0, e == 7))
            def _():
                ag_relay(1, 0).wait_recv()
                ag_relay(1, 1).wait_recv()
                ag_pair(1, 2).start()

            @pl.when(jnp.logical_and(m == 1, e == 0))
            def _():
                for step in (1, 3):
                    for h in range(2):
                        shard_wait(lax.rem(z + step, 4) * 2 + h)
                for k in range(2):
                    shard_relay(k).start()

            @pl.when(jnp.logical_and(m == 1, e == 4))
            def _():
                turn(0)
            ffn(e, local_experts * (1 + m) + e, 4 + 6 * m, 6)
            return carry
        lax.fori_loop(0, local_experts, ffn_far, 0)

        @pl.when(m == 1)
        def _():
            for h in range(2):
                shard_wait(lax.rem(z + 2, 4) * 2 + h)
            shared_load(lambda c: c.start())

        def combine_far(i, carry):
            n = 3 * m + i
            k = lax.rem(n, 2)
            slot = 3 * i * i - 5 * i + 4

            @pl.when(n >= 2)
            def _():
                pair_copy(n - 2).wait_send()
            combine(2 + 6 * m + slot + 1, slot + 1, m, pair_out.at[k], False)

            @pl.when(n >= 2)
            def _():
                pl.semaphore_wait(pair_free, 1)
            pair_copy(n).start()
            combine(2 + 6 * m + slot, slot, m, sums.at[m, i], False)
            pair_copy(n).wait_recv()
            add_into(sums.at[m, i], pair_in.at[k])
            pl.semaphore_signal(pair_free, inc=1, device_id=on_x(0, 1), device_id_type=MESH)

            @pl.when(i == 0)
            def _():
                rs_turn(m, 0).start()
                rs_turn(m, 1).start()

            @pl.when(i == 1)
            def _():
                rs_last(m, 0).start()

            @pl.when(i == 2)
            def _():
                rs_last(m, 1).start()
            return carry
        lax.fori_loop(0, 3, combine_far, 0)
        return carry

    lax.fori_loop(0, 2, far, 0)

    shared_load(lambda c: c.wait())

    def finish(m, carry):
        n = 6 + m
        k = lax.rem(n, 2)
        pair_copy(n - 2).wait_send()
        shared(2 * m + 1, pair_out.at[k])
        combine(2 * m + 1, 1, m, pair_out.at[k], True)
        pl.semaphore_wait(pair_free, 1)
        pair_copy(n).start()
        shared(2 * m, sums.at[m, 3])
        combine(2 * m, 0, m, sums.at[m, 3], True)

        @pl.when(m == 0)
        def _():
            turn(1)
        pair_copy(n).wait_recv()
        add_into(sums.at[m, 3], pair_in.at[k])
        return carry
    lax.fori_loop(0, 2, finish, 0)

    step = min(32, tok)
    for m, out in enumerate((out_a, out_b)):
        for k in (0, 2, 1, 3):
            rs_last(m, k).wait_recv()

        def write(i, carry):
            part = pl.ds(pl.multiple_of(i * step, step), step)
            total = near[2 * m, part, :].astype(F32) + sums[m, 3, part, :]
            out[part, :] = (total + last_p[m, part, :] + last_m[m, part, :]).astype(BF16)
            return carry
        lax.fori_loop(0, tok // step, write, 0)

    for m in range(2):
        for k in range(4):
            ag_own(m, k).wait_send()
            rs_last(m, k).wait_send()
        for k in range(2):
            ag_relay(m, k).wait_send()
            rs_turn(m, k).wait_send()
        for k in range(3):
            ag_pair(m, k).wait_send()
        near_pair(m).wait_send()
        pair_copy(6 + m).wait_send()
    for dx, other in others:
        meta_send(dx, other).wait_send()

    @pl.when(mine)
    def _():
        for k in range(3):
            shard_y(k).wait_send()
    for k in range(4):
        shard_z(k).wait_send()
    for k in range(2):
        shard_relay(k).wait_send()


def solution(mesh):
    ep_size = mesh.shape['ep']
    tok_spec = P(('data', 'ep', 'tp'), None)
    in_specs = (tok_spec,) * 8 + (P(None, 'tp'), P(None, 'tp'), P('tp', None), P('ep', None, None), P('ep', None, None), P('ep', None, None))

    def layer_local(tokens_a, tokens_b, experts_a, experts_b, gates_a, gates_b, slots_a, slots_b, shared_w1, shared_w3, shared_w2, routed_w1, routed_w3, routed_w2):
        tok, top_k = experts_a.shape
        local_experts, model_dim, ff = routed_w1.shape
        shard = shared_w2.shape[0]
        cap = max(4, (2 * tok * top_k) // (local_experts * ep_size))
        half = tok // 2
        f_tiles, n_tiles = ff // 128, model_dim // 256

        def row_of(experts, slots):
            return jnp.where(slots >= 0, experts * cap + slots, -1).astype(F32)

        meta = jnp.stack([row_of(experts_a, slots_a), gates_a, row_of(experts_b, slots_b), gates_b])
        meta = jnp.pad(meta.transpose(0, 2, 1), ((0, 0), (0, 8 - top_k), (0, 0)))
        shared_in = jnp.stack([shared_w1.T, shared_w3.T, shared_w2])

        hbm = pl.BlockSpec(memory_space=pl.ANY)
        vmem = pl.BlockSpec(memory_space=pltpu.VMEM)
        dma = pltpu.SemaphoreType.DMA
        row_count = local_experts * cap * ep_size
        flops = 2 * row_count * model_dim * ff * 6 + 4 * tok * model_dim * ff * 6
        out_a, out_b, _, _ = pl.pallas_call(
            functools.partial(_layer_kernel, cap, top_k),
            out_shape=(
                jax.ShapeDtypeStruct((tok, model_dim), BF16),
                jax.ShapeDtypeStruct((tok, model_dim), BF16),
                jax.ShapeDtypeStruct((2, 8, tok, model_dim), BF16),
                jax.ShapeDtypeStruct((8, 3, shard, model_dim), BF16),
            ),
            in_specs=[hbm] * 7,
            out_specs=(vmem, vmem, hbm, hbm),
            scratch_shapes=[
                pltpu.VMEM((4, tok, model_dim), BF16),
                pltpu.VMEM((2, tok, model_dim), BF16),
                pltpu.VMEM((8, 4, 8, tok), F32),
                pltpu.VMEM((local_experts, 16, cap, model_dim), BF16),
                pltpu.VMEM((2, f_tiles, model_dim, 256), BF16),
                pltpu.VMEM((2, ff, model_dim), BF16),
                pltpu.VMEM((max(6 * cap, tok), ff), BF16),
                pltpu.VMEM((2, tok, model_dim), F32),
                pltpu.VMEM((2, tok, model_dim), F32),
                pltpu.VMEM((2, 4, tok, model_dim), F32),
                pltpu.VMEM((2, half, model_dim), F32),
                pltpu.VMEM((2, half, model_dim), F32),
                pltpu.VMEM((2, tok, model_dim), F32),
                pltpu.VMEM((2, tok, model_dim), F32),
                dma((4,)), dma((2,)), dma((8,)), dma((8,)), dma((2, 9)), dma((2, 9)), dma((2,)), dma((2, 2 * f_tiles + 1)),
                dma((9,)), dma((8,)), dma, dma((8, 2 + n_tiles)), dma((8,)), dma((8,)), dma((2, 6)), dma((2, 6)),
                pltpu.SemaphoreType.REGULAR,
            ],
            compiler_params=pltpu.CompilerParams(collective_id=0, has_side_effects=True, vmem_limit_bytes=67_000_000),
            cost_estimate=pl.CostEstimate(flops=flops, bytes_accessed=200_000_000, transcendentals=0),
        )(tokens_a, tokens_b, meta, shared_in, routed_w1, routed_w3, routed_w2)
        return (out_a, out_b)

    return jax.shard_map(layer_local, mesh=mesh, in_specs=in_specs, out_specs=(tok_spec, tok_spec), check_vma=False)
```

time: 654 us -> 176 us (0.27)
  waiting for transfers between devices: 347 us -> 0 us
  Pallas kernels: 0 us -> 166 us
  matrix products: 135 us -> 0 us
  local copies, waits for them, and re-layouts: 92.5 us -> 4.55 us
  other arithmetic: 34.5 us -> 3.61 us
  starting transfers between devices: 24.9 us -> 0 us
  between operations: 14.7 us -> 0.64 us
    all_to_all x4 -> x0, waiting for transfers between devices: 203 us -> none  [the longest x2 111 us: routed_path(): lax.all_to_all(send_rows.reshape(local_experts, ep_size, cap_rows, model_...]
    pallas_call x0 -> x1, Pallas kernels: none -> 166 us  [layer_local(): pl.pallas_call(functools.partial(_layer_kernel, cap, top_k), out_shape=(j...]
    all_gather x2 -> x0, waiting for transfers between devices: 142 us -> none  [shared_path(): gathered = lax.all_gather(x_local, 'tp', axis=0, tiled=True)]
    dot_general x10 -> x0, matrix products: 135 us -> none  [the longest x2 51.2 us: routed_path(): jnp.einsum('erf,efd->erd', hidden, routed_w2, preferred_element_type=jnp....]
    gather x4 -> x0, local copies, waits for them, and re-layouts: 40.8 us -> none  [routed_path(): jnp.take(back_rows.reshape(num_rows, model_dim), jnp.maximum(row_ids, 0),...]
    all_to_all x4 -> x0, starting transfers between devices: 24.3 us -> none  [the longest x2 12.4 us: routed_path(): lax.all_to_all(expert_out.reshape(local_experts, ep_size, cap_rows, model...]
    all_to_all x4 -> x0, local copies, waits for them, and re-layouts: 21.9 us -> none  [the longest x2 14.2 us: routed_path(): lax.all_to_all(expert_out.reshape(local_experts, ep_size, cap_rows, model...]
    reshape x4 -> x0, local copies, waits for them, and re-layouts: 21.6 us -> none  [the longest x2 14.1 us: routed_path(): expert_out.reshape(local_experts, ep_size, cap_rows, model_dim)]
  transfers between devices with their start and end apart: 8 -> 0, of which waited for: 6 -> 0; matrix products, arithmetic and copies ran while one was open for 39% -> 0% of each run, Pallas kernels for 0% -> 0%
where the time goes in v1:
time: 176 us; the launch traced here: 175 us
  Pallas kernels  166 us (94%)
  local copies, waits for them, and re-layouts  4.55 us (3%)
  other arithmetic  3.61 us (2%)
    pallas_call x1, Pallas kernels, layer_local(): pl.pallas_call(functools.partial(_layer_kernel, cap, top_k), out_shape=(j...  166 us
    unnamed x2, local copies, waits for them, and re-layouts  3.93 us

profile of v1, /device:TPU:1, one launch (start us, length us, event | category | flops | bytes accessed | tf_op | source)
XLA Modules:
  0.0 174.9 jit_solution(5691394079126989419)
XLA Ops:
  0.6 0.8 convert_bitcast_fusion
  1.4 0.7 maximum_bitcast_fusion
  2.1 0.6 pad.4.meta_in
  2.7 2.1 %pad_maximum_fusion.shared_in = bf16[3,112,1280]{2,1,0:T(8,128)(2,1)} fusion(bf16[1,112,1280]{2,1,0:T(8,128)(2,1)} %bitcast.15, bf16[1,112,1280]{2,1,0:T(8,128)(2,1)} %bitcast.16, bf16[1,112,1280]{2,1,0:T(8,128)(2,1)} %bitcast.17), kind=kLoop, calls=%fused_computation | loop fusion | flops 860160 | bytes 1720320 | tf_op jit(solution)/shard_map/stack | solution.py:462
  4.9 166.1 %shard_map.149 = (bf16[256,1280]{1,0:T(8,128)(2,1)}, bf16[256,1280]{1,0:T(8,128)(2,1)}, bf16[2,8,256,1280]{3,2,1,0:T(8,128)(2,1)}, bf16[8,3,112,1280]{3,2,1,0:T(8,128)(2,1)}) custom-call(bf16[256,1280]{1,0:T(8,128)(2,1)} %tok_a.1, bf16[256,1280]{1,0:T(8,128)(2,1)} %tok_b.1, f32[4,8,256]{2,1,0:T(8,128)} %pad.4.meta_in, ...), custom_call_target="tpu_custom_call" | custom-call | flops 49325015040 | bytes 200000000 | tf_op jit(solution)/shard_map/pallas_call | solution.py:469
  170.9 2.0 %copy.18 = bf16[256,1280]{1,0:T(8,128)(2,1)} copy(bf16[256,1280]{1,0:T(8,128)(2,1)} %get-tuple-element.10) | data formatting | bytes 1310720
  172.9 2.0 %copy.19 = bf16[256,1280]{1,0:T(8,128)(2,1)} copy(bf16[256,1280]{1,0:T(8,128)(2,1)} %get-tuple-element.11) | data formatting | bytes 1310720

commit v2 on v1

v2 whole, which is shorter than its diff:
```python
import functools

import jax
import jax.numpy as jnp
from jax import lax
from jax.experimental import pallas as pl
from jax.experimental.pallas import tpu as pltpu
from jax.sharding import PartitionSpec as P

MESH = pl.DeviceIdType.MESH
F32 = jnp.float32
BF16 = jnp.bfloat16
ORDER = (0, 2, 1, 3)


def _split_gate(gate):
    high = gate.astype(BF16)
    rest = gate - high.astype(F32)
    middle = rest.astype(BF16)
    low = (rest - middle.astype(F32)).astype(BF16)
    return high, middle, low


def _layer_kernel(
    cap, top_k,
    tok_a, tok_b, exp_a, exp_b, gate_a, gate_b, slot_a, slot_b, shared_w1, shared_w3, shared_w2, routed_w1, routed_w3, routed_w2,
    out_a, out_b, far_hbm, gath_hbm,
    near, stage, meta, rows, w1, w3, w2, hid, pair_out, pair_in, sums, turn_p, turn_m, last_p, last_m, shard_vmem,
    sem_near, sem_near_recv, sem_meta_send, sem_meta_recv, sem_ag_send, sem_ag_recv, sem_stage, sem_w,
    sem_sh_send, sem_sh_recv, sem_sh_own, sem_sh_load, sem_pair_send, sem_pair_recv, sem_rs_send, sem_rs_recv, sem_out, pair_free,
):
    local_experts, model_dim, ff = routed_w1.shape
    tok = tok_a.shape[0]
    half = tok // 2
    shard = shared_w2.shape[0]
    num_rows = local_experts * cap
    tile = 256
    n_tiles = model_dim // tile
    f_tiles = ff // 128

    ep = lax.axis_index('ep')
    tp = lax.axis_index('tp')
    chip, core = ep // 2, lax.rem(ep, 2)
    z, y = tp // 4, lax.rem(tp, 4)

    def on_x(step, other=0):
        side = core if other == 0 else 1 - core
        return {'ep': lax.rem(chip + step, 4) * 2 + side, 'tp': tp}

    def on_y(step):
        return {'ep': ep, 'tp': z * 4 + lax.rem(y + step, 4)}

    def on_z(step):
        return {'ep': ep, 'tp': lax.rem(z + step, 4) * 4 + y}

    def remote(src, dst, send, recv, device):
        return pltpu.make_async_remote_copy(src_ref=src, dst_ref=dst, send_sem=send, recv_sem=recv, device_id=device, device_id_type=MESH)

    low, high = pl.ds(0, half), pl.ds(half, half)

    tokens = (tok_a, tok_b)

    def ag_own(m, k):
        part, step, slot = ((low, 1, 6), (high, 1, 6), (high, 3, 2), (low, 3, 2))[k]
        return remote(tokens[m].at[part], far_hbm.at[m, slot, part], sem_ag_send.at[m, k], sem_ag_recv.at[m, k], on_x(step))

    def ag_relay(m, k):
        part, step, slot = ((low, 1, 6), (high, 3, 2))[k]
        return remote(far_hbm.at[m, slot, part], far_hbm.at[m, 4, part], sem_ag_send.at[m, 4 + k], sem_ag_recv.at[m, 4 + k], on_x(step))

    def ag_pair(m, k):
        slot = (6, 2, 4)[k]
        return remote(far_hbm.at[m, slot], far_hbm.at[m, slot + 1], sem_ag_send.at[m, 6 + k], sem_ag_recv.at[m, 6 + k], on_x(0, 1))

    def near_pair(m):
        return remote(tokens[m], near.at[2 * m + 1], sem_near.at[m], sem_near_recv.at[m], on_x(0, 1))

    def near_own(m):
        return pltpu.make_async_copy(tokens[m], near.at[2 * m], sem_near.at[2 + m])

    def meta_send(dx, other):
        back = (4 - dx) % 4
        slot = back * 2 + other
        return remote(meta.at[0], meta.at[slot], sem_meta_send.at[dx * 2 + other], sem_meta_recv.at[slot], on_x(dx, other))

    others = [(dx, other) for dx in range(4) for other in range(2) if (dx, other) != (0, 0)]

    mine = lax.rem(y, 2) == core
    own_slot = z * 2 + y // 2

    def shard_y(k):
        return remote(shard_vmem, gath_hbm.at[own_slot], sem_sh_send.at[k], sem_sh_recv.at[own_slot], on_y((1, 3, 2)[k]))

    shard_in = [pltpu.make_async_copy(w, shard_vmem.at[i], sem_sh_own.at[i]) for i, w in enumerate((shared_w1, shared_w3, shared_w2))]
    shard_own = pltpu.make_async_copy(shard_vmem, gath_hbm.at[own_slot], sem_sh_own.at[3])

    def shard_wait(slot):
        pltpu.make_async_copy(shard_vmem, gath_hbm.at[slot], sem_sh_recv.at[slot]).wait()

    def shard_z(k):
        slot = z * 2 + k % 2
        return remote(gath_hbm.at[slot], gath_hbm.at[slot], sem_sh_send.at[3 + k], sem_sh_recv.at[slot], on_z((1, 3)[k // 2]))

    def shard_relay(k):
        slot = lax.rem(z + (3, 1)[k], 4) * 2 + k
        return remote(gath_hbm.at[slot], gath_hbm.at[slot], sem_sh_send.at[7 + k], sem_sh_recv.at[slot], on_z((1, 3)[k]))

    def weights_in(buf, expert, act):
        act(pltpu.make_async_copy(routed_w1.at[expert], w1.at[buf], sem_w.at[buf, 0]))
        act(pltpu.make_async_copy(routed_w3.at[expert], w3.at[buf], sem_w.at[buf, 1]))

    def weights_out(buf, expert, act):
        act(pltpu.make_async_copy(routed_w2.at[expert], w2.at[buf], sem_w.at[buf, 2]))

    def pair_copy(n):
        k = lax.rem(n, 2)
        return remote(pair_out.at[k], pair_in.at[k], sem_pair_send.at[n], sem_pair_recv.at[n], on_x(0, 1))

    def rs_turn(m, k):
        part, step, dst = ((low, 1, turn_p), (high, 3, turn_m))[k]
        return remote(sums.at[m, 0, part], dst.at[m], sem_rs_send.at[m, k], sem_rs_recv.at[m, k], on_x(step))

    def rs_last(m, k):
        part, step, dst, i = ((high, 1, last_m, 1), (low, 3, last_p, 2), (low, 1, last_m, 1), (high, 3, last_p, 2))[k]
        return remote(sums.at[m, i, part], dst.at[m, part], sem_rs_send.at[m, 2 + k], sem_rs_recv.at[m, 2 + k], on_x(step))

    def hits_of(slot, m):
        ids = meta[slot, 2 * m] - (ep * num_rows).astype(F32)
        row = lax.broadcasted_iota(jnp.int32, (num_rows, tok), 0).astype(F32)
        return [row == ids[j:j + 1, :] for j in range(top_k)]

    def place(q, slot, m, src, src_index):
        hits = hits_of(slot, m)
        matrix = functools.reduce(jnp.logical_or, hits)
        matrix = jnp.where(matrix, 1.0, 0.0).astype(BF16)
        for n in range(n_tiles):
            col = pl.ds(n * tile, tile)
            picked = jnp.dot(matrix, src[src_index, :, col], preferred_element_type=F32).astype(BF16)
            rows[:, q, :, col] = picked.reshape(local_experts, cap, tile)

    def ffn(expert, count, q0, nq, first=True, last=True):
        buf = lax.rem(count, 2)
        if first:
            weights_in(buf, expert, lambda c: c.wait())
        size = nq * cap
        x = rows[expert, pl.ds(q0, nq)].reshape(size, model_dim)
        for j in range(f_tiles):
            col = pl.ds(128 * j, 128)
            weight = jnp.concatenate([w1[buf, :, col], w3[buf, :, col]], axis=1)
            both = jnp.dot(x, weight, preferred_element_type=F32)
            hid[pl.ds(0, size), col] = (jax.nn.silu(both[:, :128]) * both[:, 128:]).astype(BF16)

        @pl.when(jnp.logical_and(last, count + 2 < 3 * local_experts))
        def _():
            weights_in(buf, lax.rem(expert + 2, local_experts), lambda c: c.start())

        if first:
            weights_out(buf, expert, lambda c: c.wait())
        h = hid[pl.ds(0, size), :]
        for n in range(n_tiles):
            col = pl.ds(n * tile, tile)
            res = jnp.dot(h, w2[buf, :, col], preferred_element_type=F32).astype(BF16)
            rows[expert, pl.ds(q0, nq), :, col] = res.reshape(nq, cap, tile)

        @pl.when(jnp.logical_and(last, count + 2 < 3 * local_experts))
        def _():
            weights_out(buf, lax.rem(expert + 2, local_experts), lambda c: c.start())

    def combine(q, slot, m, dst, add):
        gates = meta[slot, 2 * m + 1]
        matrix = 0.0
        for j, hit in enumerate(hits_of(slot, m)):
            matrix = matrix + jnp.where(hit, gates[j:j + 1, :], 0.0)
        matrix = jnp.concatenate(_split_gate(matrix), axis=0)
        for n in range(n_tiles):
            col = pl.ds(n * tile, tile)
            res = rows[:, q, :, col].reshape(num_rows, tile)
            res = jnp.concatenate([res, res, res], axis=0)
            part = lax.dot_general(matrix, res, (((0,), (0,)), ((), ())), preferred_element_type=F32)
            dst[:, col] = dst[:, col] + part if add else part

    def add_into(dst, src):
        step = min(32, dst.shape[0])

        def body(i, carry):
            part = pl.ds(pl.multiple_of(i * step, step), step)
            dst[part, :] = dst[part, :] + src[part, :]
            return carry
        lax.fori_loop(0, dst.shape[0] // step, body, 0)

    def shared_piece(p):
        return w1[p // f_tiles, pl.ds(0, ff), pl.ds(128 * (p % f_tiles), 128)]

    def shared(q, dst):
        x = near[q]
        width = min(tile, ff)
        dims = (((1,), (1,)), ((), ()))
        for start in range(0, ff, width):
            size = min(width, ff - start)
            row = pl.ds(start, size)
            a = lax.dot_general(x, w2[0, row, :], dims, preferred_element_type=F32)
            g = lax.dot_general(x, w2[1, row, :], dims, preferred_element_type=F32)
            hid[pl.ds(0, tok), row] = (jax.nn.silu(a) * g).astype(BF16)
        h = hid[pl.ds(0, tok), :]
        for n in range(n_tiles):
            weight = jnp.concatenate([shared_piece(2 * n), shared_piece(2 * n + 1)], axis=1)
            dst[:, pl.ds(n * tile, tile)] = jnp.dot(h, weight, preferred_element_type=F32)

    def shared_load(act):
        def body(k, carry):
            row = pl.ds(pl.multiple_of(k * shard, shard), shard)
            act(pltpu.make_async_copy(gath_hbm.at[k, 0], w2.at[0, row], sem_sh_load.at[k, 0]))
            act(pltpu.make_async_copy(gath_hbm.at[k, 1], w2.at[1, row], sem_sh_load.at[k, 1]))
            act(pltpu.make_async_copy(gath_hbm.at[k, 2, :, pl.ds(0, ff)], w1.at[0, row], sem_sh_load.at[k, 2]))
            rest = pl.ds(0, model_dim - ff)
            act(pltpu.make_async_copy(gath_hbm.at[k, 2, :, pl.ds(ff, model_dim - ff)], w1.at[1, row, rest], sem_sh_load.at[k, 3]))
            return carry
        lax.fori_loop(0, 8, body, 0)

    for i in range(2):
        weights_in(i, i, lambda c: c.start())
        weights_out(i, i, lambda c: c.start())
    near_own(0).start()
    near_own(1).start()
    for copy in shard_in:
        copy.start()
    for m, (experts, gates, slots) in enumerate(((exp_a, gate_a, slot_a), (exp_b, gate_b, slot_b))):
        meta[0, 2 * m] = jnp.zeros((8, tok), F32)
        meta[0, 2 * m + 1] = jnp.zeros((8, tok), F32)
        row = jnp.where(slots[...] >= 0, experts[...] * cap + slots[...], -1)
        meta[0, 2 * m, pl.ds(0, top_k), :] = row.astype(F32)
        meta[0, 2 * m + 1, pl.ds(0, top_k), :] = gates[...]
    barrier = pltpu.get_barrier_semaphore()
    peers = [on_x(dx, other) for dx, other in others] + [on_y(1), on_y(2), on_y(3), on_z(1), on_z(3)]
    for peer in peers:
        pl.semaphore_signal(barrier, inc=1, device_id=peer, device_id_type=MESH)
    pl.semaphore_wait(barrier, len(peers))

    for k in ORDER:
        ag_own(0, k).start()
    near_pair(0).start()
    near_pair(1).start()
    for dx, other in others:
        meta_send(dx, other).start()

    for copy in shard_in:
        copy.wait()

    @pl.when(mine)
    def _():
        for k in range(3):
            shard_y(k).start()
        shard_own.start()

    near_own(0).wait()
    near_own(1).wait()

    def place_near(i, carry):
        @pl.when(i == 2)
        def _():
            near_pair(0).wait_recv()
            near_pair(1).wait_recv()
            meta_send(0, 1).wait_recv()
        q = 2 * lax.rem(i, 2) + i // 2
        place(q, i // 2, lax.rem(i, 2), near, q)
        return carry
    lax.fori_loop(0, 4, place_near, 0)

    def ffn_near(e, carry):
        @pl.when(e == 2)
        def _():
            ag_own(0, 0).wait_recv()
            ag_relay(0, 0).start()
            ag_own(0, 2).wait_recv()
            ag_relay(0, 1).start()
            for k in ORDER:
                ag_own(1, k).start()

        @pl.when(e == 7)
        def _():
            ag_own(0, 1).wait_recv()
            ag_pair(0, 0).start()
            ag_own(0, 3).wait_recv()
            ag_pair(0, 1).start()
        ffn(e, e, 0, 4)
        return carry
    lax.fori_loop(0, local_experts, ffn_near, 0)

    for dx, other in others[1:]:
        meta_send(dx, other).wait_recv()

    def shards_on():
        for h in range(2):
            owned = jnp.logical_and(mine, y // 2 == h)

            @pl.when(owned)
            def _():
                shard_own.wait()

            @pl.when(jnp.logical_not(owned))
            def _():
                shard_wait(z * 2 + h)
        for k in range(4):
            shard_z(k).start()

    def turn(m):
        rs_turn(m, 0).wait_recv()
        add_into(sums.at[m, 1, low], turn_p.at[m])
        rs_last(m, 2).start()
        rs_turn(m, 1).wait_recv()
        add_into(sums.at[m, 2, high], turn_m.at[m])
        rs_last(m, 3).start()

    def far_slot(i):
        return jnp.where(i < 4, 2 + 4 * lax.rem(i, 2) + i // 2, i)

    def stage_copy(m, i):
        k = lax.rem(i, 4)
        return pltpu.make_async_copy(far_hbm.at[m, far_slot(i)], stage.at[k], sem_stage.at[k])

    def far_opposite(m):
        ag_relay(m, 0).wait_recv()
        ag_relay(m, 1).wait_recv()
        ag_pair(m, 2).start()

    def far(m, carry):
        def place_far(i, carry):
            stage_copy(m, i).wait()
            slot = far_slot(i)
            order = jnp.where(i < 4, 2 * lax.rem(i, 2) + i // 2, i)
            place(4 + 6 * m + order, slot, m, stage, lax.rem(i, 4))
            return carry

        stage_copy(m, 0).start()
        stage_copy(m, 1).start()
        ag_pair(m, 1).wait_recv()
        ag_pair(m, 0).wait_recv()
        stage_copy(m, 2).start()
        stage_copy(m, 3).start()
        lax.fori_loop(0, 4, place_far, 0)

        @pl.when(m == 0)
        def _():
            far_opposite(0)
        stage_copy(m, 4).start()
        ag_pair(m, 2).wait_recv()
        stage_copy(m, 5).start()
        lax.fori_loop(4, 6, place_far, 0)

        def ffn_far(e, carry):
            @pl.when(jnp.logical_and(m == 0, e == 0))
            def _():
                shards_on()

            @pl.when(jnp.logical_and(m == 0, e == 2))
            def _():
                ag_own(1, 0).wait_recv()
                ag_relay(1, 0).start()
                ag_own(1, 2).wait_recv()
                ag_relay(1, 1).start()

            @pl.when(jnp.logical_and(m == 0, e == 6))
            def _():
                ag_own(1, 1).wait_recv()
                ag_pair(1, 0).start()
                ag_own(1, 3).wait_recv()
                ag_pair(1, 1).start()

            @pl.when(jnp.logical_and(m == 0, e == 7))
            def _():
                far_opposite(1)

            @pl.when(jnp.logical_and(m == 1, e == 3))
            def _():
                turn(0)

            @pl.when(jnp.logical_and(m == 1, e == 6))
            def _():
                for step in (1, 3):
                    for h in range(2):
                        shard_wait(lax.rem(z + step, 4) * 2 + h)
                for k in range(2):
                    shard_relay(k).start()
            ffn(e, local_experts * (1 + m) + e, 4 + 6 * m, 6)
            return carry
        lax.fori_loop(0, local_experts, ffn_far, 0)

        slots, orders = (4, 2, 6), (4, 0, 2)

        def other(i):
            n = 3 * m + i
            k = lax.rem(n, 2)

            @pl.when(n >= 2)
            def _():
                pair_copy(n - 2).wait_send()
            combine(4 + 6 * m + orders[i] + 1, slots[i] + 1, m, pair_out.at[k], False)

            @pl.when(n >= 2)
            def _():
                pl.semaphore_wait(pair_free, 1)
            pair_copy(n).start()

        def same(i):
            combine(4 + 6 * m + orders[i], slots[i], m, sums.at[m, i], False)

        def complete(i):
            n = 3 * m + i
            pair_copy(n).wait_recv()
            add_into(sums.at[m, i], pair_in.at[lax.rem(n, 2)])
            pl.semaphore_signal(pair_free, inc=1, device_id=on_x(0, 1), device_id_type=MESH)
            if i == 0:
                rs_turn(m, 0).start()
                rs_turn(m, 1).start()
            else:
                rs_last(m, i - 1).start()

        other(0)
        other(1)
        same(0)
        complete(0)
        other(2)
        same(1)
        complete(1)
        same(2)
        complete(2)
        return carry

    lax.fori_loop(0, 2, far, 0)

    for h in range(2):
        shard_wait(lax.rem(z + 2, 4) * 2 + h)
    shared_load(lambda c: c.start())
    shared_load(lambda c: c.wait())

    def finish(m, carry):
        n = 6 + m
        k = lax.rem(n, 2)
        pair_copy(n - 2).wait_send()
        shared(2 * m + 1, pair_out.at[k])
        combine(2 * m + 1, 1, m, pair_out.at[k], True)
        pl.semaphore_wait(pair_free, 1)
        pair_copy(n).start()
        shared(2 * m, sums.at[m, 3])
        combine(2 * m, 0, m, sums.at[m, 3], True)

        @pl.when(m == 0)
        def _():
            turn(1)
        pair_copy(n).wait_recv()
        add_into(sums.at[m, 3], pair_in.at[k])
        return carry
    lax.fori_loop(0, 2, finish, 0)

    def out_copy(m, k):
        part = (low, high)[k]
        return pltpu.make_async_copy(near.at[2 * m, part], (out_a, out_b)[m].at[part], sem_out.at[m, k])

    step = min(32, half)
    for m in range(2):
        for k in ORDER:
            rs_last(m, k).wait_recv()

        def write(i, carry):
            part = pl.ds(pl.multiple_of(i * step, step), step)
            total = near[2 * m, part, :].astype(F32) + sums[m, 3, part, :]
            near[2 * m, part, :] = (total + last_p[m, part, :] + last_m[m, part, :]).astype(BF16)
            return carry
        for k in range(2):
            lax.fori_loop(k * half // step, (k + 1) * half // step, write, 0)
            out_copy(m, k).start()

    for m in range(2):
        for k in range(2):
            out_copy(m, k).wait()
        for k in range(4):
            ag_own(m, k).wait_send()
            rs_last(m, k).wait_send()
        for k in range(2):
            ag_relay(m, k).wait_send()
            rs_turn(m, k).wait_send()
        for k in range(3):
            ag_pair(m, k).wait_send()
        near_pair(m).wait_send()
        pair_copy(6 + m).wait_send()
    for dx, other in others:
        meta_send(dx, other).wait_send()

    @pl.when(mine)
    def _():
        for k in range(3):
            shard_y(k).wait_send()
    for k in range(4):
        shard_z(k).wait_send()
    for k in range(2):
        shard_relay(k).wait_send()


def _move_kernel(in_a, in_b, out_a, out_b, held, sem):
    half = in_a.shape[0] // 2
    copies = []
    for m, (src, dst) in enumerate(((in_a, out_a), (in_b, out_b))):
        for k in range(2):
            part = pl.ds(k * half, half)
            copies.append((
                pltpu.make_async_copy(src.at[part], held.at[m, part], sem.at[0, m, k]),
                pltpu.make_async_copy(held.at[m, part], dst.at[part], sem.at[1, m, k]),
            ))
    for fetch, _ in copies:
        fetch.start()
    for fetch, store in copies:
        fetch.wait()
        store.start()
    for _, store in copies:
        store.wait()


def solution(mesh):
    ep_size = mesh.shape['ep']
    tok_spec = P(('data', 'ep', 'tp'), None)
    columns, experts = P(None, 'tp'), P('ep', None, None)
    in_specs = (tok_spec,) * 8 + (columns, columns, P('tp', None), experts, experts, experts)

    def layer_local(tokens_a, tokens_b, experts_a, experts_b, gates_a, gates_b, slots_a, slots_b, shared_w1, shared_w3, shared_w2, routed_w1, routed_w3, routed_w2):
        tok, top_k = experts_a.shape
        local_experts, model_dim, ff = routed_w1.shape
        shard = shared_w2.shape[0]
        cap = max(4, (2 * tok * top_k) // (local_experts * ep_size))
        half = tok // 2

        hbm = pl.BlockSpec(memory_space=pl.ANY)
        dma = pltpu.SemaphoreType.DMA
        four, eight = dma((4,)), dma((8,))
        out_a, out_b, _, _ = pl.pallas_call(
            functools.partial(_layer_kernel, cap, top_k),
            out_shape=(
                jax.ShapeDtypeStruct((tok, model_dim), BF16),
                jax.ShapeDtypeStruct((tok, model_dim), BF16),
                jax.ShapeDtypeStruct((2, 8, tok, model_dim), BF16),
                jax.ShapeDtypeStruct((8, 3, shard, model_dim), BF16),
            ),
            in_specs=[hbm] * 2 + [pl.BlockSpec(memory_space=pltpu.VMEM)] * 6 + [hbm] * 6,
            out_specs=(hbm, hbm, hbm, hbm),
            scratch_shapes=[
                pltpu.VMEM((4, tok, model_dim), BF16),
                pltpu.VMEM((4, tok, model_dim), BF16),
                pltpu.VMEM((8, 4, 8, tok), F32),
                pltpu.VMEM((local_experts, 16, cap, model_dim), BF16),
                pltpu.VMEM((2, model_dim, ff), BF16),
                pltpu.VMEM((2, model_dim, ff), BF16),
                pltpu.VMEM((2, ff, model_dim), BF16),
                pltpu.VMEM((max(6 * cap, tok), ff), BF16),
                pltpu.VMEM((2, tok, model_dim), F32),
                pltpu.VMEM((2, tok, model_dim), F32),
                pltpu.VMEM((2, 4, tok, model_dim), F32),
                pltpu.VMEM((2, half, model_dim), F32),
                pltpu.VMEM((2, half, model_dim), F32),
                pltpu.VMEM((2, tok, model_dim), F32),
                pltpu.VMEM((2, tok, model_dim), F32),
                pltpu.VMEM((3, shard, model_dim), BF16),
                four, dma((2,)), eight, eight, *[dma((2, 9))] * 2, four, dma((2, 3)),
                dma((9,)), eight, four, dma((8, 4)), eight, eight, *[dma((2, 6))] * 2, dma((2, 2)),
                pltpu.SemaphoreType.REGULAR,
            ],
            compiler_params=pltpu.CompilerParams(collective_id=0, has_side_effects=True, vmem_limit_bytes=67_000_000),
        )(tokens_a, tokens_b, experts_a.T, experts_b.T, gates_a.T, gates_b.T, slots_a.T, slots_b.T, shared_w1.T, shared_w3.T, shared_w2, routed_w1, routed_w3, routed_w2)
        return pl.pallas_call(
            _move_kernel,
            out_shape=(jax.ShapeDtypeStruct((tok, model_dim), BF16),) * 2,
            in_specs=[hbm] * 2,
            out_specs=(hbm, hbm),
            scratch_shapes=[pltpu.VMEM((2, tok, model_dim), BF16), dma((2, 2, 2))],
            compiler_params=pltpu.CompilerParams(vmem_limit_bytes=66_000_000),
        )(out_a, out_b)

    return jax.shard_map(layer_local, mesh=mesh, in_specs=in_specs, out_specs=(tok_spec, tok_spec), check_vma=False)
```

time: 176 us -> 156 us (0.89)
  Pallas kernels: 166 us -> 155 us
  local copies, waits for them, and re-layouts: 4.55 us -> 0 us
  other arithmetic: 3.61 us -> 0 us
    pallas_call x1, Pallas kernels: 166 us -> 153 us  [layer_local(): pl.pallas_call(functools.partial(_layer_kernel, cap, top_k), out_shape=(j...]
    unnamed x2 -> x0, local copies, waits for them, and re-layouts: 3.93 us -> none
    another operation x2 -> x0, other arithmetic: 2.89 us -> none  [the longest x1 2.14 us: layer_local(): shared_in = jnp.stack([shared_w1.T, shared_w3.T, shared_w2])]
    pallas_call x0 -> x1, Pallas kernels: none -> 2.09 us  [layer_local(): pl.pallas_call(_move_kernel, out_shape=(jax.ShapeDtypeStruct((tok, model_...]
where the time goes in v2:
time: 156 us
  Pallas kernels  155 us (99%)
    pallas_call x1, Pallas kernels, layer_local(): pl.pallas_call(functools.partial(_layer_kernel, cap, top_k), out_shape=(j...  153 us

profile of v2, /device:TPU:1, one launch (start us, length us, event | category | flops | bytes accessed | tf_op | source)
XLA Modules:
  0.0 155.9 jit_solution(5268554218033042833)
XLA Ops:
  0.6 153.0 %shard_map.149 = (bf16[256,1280]{1,0:T(8,128)(2,1)}, bf16[256,1280]{1,0:T(8,128)(2,1)}, bf16[2,8,256,1280]{3,2,1,0:T(8,128)(2,1)}, bf16[8,3,112,1280]{3,2,1,0:T(8,128)(2,1)}) custom-call(bf16[256,1280]{1,0:T(8,128)(2,1)} %tok_a.1, bf16[256,1280]{1,0:T(8,128)(2,1)} %tok_b.1, s32[6,256]{1,0:T(8,128)} %bitcast.10, s32[6,256]{1,0:T(8,128)} %bitcast.11, ...), custom_call_target="tpu_custom_call" | custom-call | tf_op jit(solution)/shard_map/pallas_call | solution.py:534
  153.6 2.1 %shard_map.150 = (bf16[256,1280]{1,0:T(8,128)(2,1)}, bf16[256,1280]{1,0:T(8,128)(2,1)}) custom-call(bf16[256,1280]{1,0:T(8,128)(2,1)} %get-tuple-element.4.in_a, bf16[256,1280]{1,0:T(8,128)(2,1)} %get-tuple-element.5.in_b), custom_call_target="tpu_custom_call" | custom-call | tf_op jit(solution)/shard_map/pallas_call | solution.py:567

commit v3 on v2

--- a/solution.py
+++ b/solution.py
@@ -276,7 +276,7 @@
             for k in ORDER:
                 ag_own(1, k).start()
 
-        @pl.when(e == 7)
+        @pl.when(e == 6)
         def _():
             ag_own(0, 1).wait_recv()
             ag_pair(0, 0).start()
@@ -370,7 +370,7 @@
             def _():
                 far_opposite(1)
 
-            @pl.when(jnp.logical_and(m == 1, e == 3))
+            @pl.when(jnp.logical_and(m == 1, e == 4))
             def _():
                 turn(0)
 

time: 156 us -> 156 us (level)
  no operation moved by 1% of the time
where the time goes in v3:
time: 156 us
  Pallas kernels  155 us (99%)
    pallas_call x1, Pallas kernels, layer_local(): pl.pallas_call(functools.partial(_layer_kernel, cap, top_k), out_shape=(j...  153 us

profile of v3, /device:TPU:1, one launch (start us, length us, event | category | flops | bytes accessed | tf_op | source)
XLA Modules:
  0.0 155.9 jit_solution(13898599239326268697)
XLA Ops:
  0.6 153.0 %shard_map.149 = (bf16[256,1280]{1,0:T(8,128)(2,1)}, bf16[256,1280]{1,0:T(8,128)(2,1)}, bf16[2,8,256,1280]{3,2,1,0:T(8,128)(2,1)}, bf16[8,3,112,1280]{3,2,1,0:T(8,128)(2,1)}) custom-call(bf16[256,1280]{1,0:T(8,128)(2,1)} %tok_a.1, bf16[256,1280]{1,0:T(8,128)(2,1)} %tok_b.1, s32[6,256]{1,0:T(8,128)} %bitcast.10, s32[6,256]{1,0:T(8,128)} %bitcast.11, ...), custom_call_target="tpu_custom_call" | custom-call | tf_op jit(solution)/shard_map/pallas_call | solution.py:534
  153.6 2.1 %shard_map.150 = (bf16[256,1280]{1,0:T(8,128)(2,1)}, bf16[256,1280]{1,0:T(8,128)(2,1)}) custom-call(bf16[256,1280]{1,0:T(8,128)(2,1)} %get-tuple-element.4.in_a, bf16[256,1280]{1,0:T(8,128)(2,1)} %get-tuple-element.5.in_b), custom_call_target="tpu_custom_call" | custom-call | tf_op jit(solution)/shard_map/pallas_call | solution.py:567
